TPU v7x, 32 devices: a whole 2x2x4 slice. The times are simulated.
32 devices in a mesh: grp: 2 (over x), sub: 16 (over z, y, core).
Axes of the slice: x: 2, y: 2, z: 4, core: 2. Of those that a mesh axis runs over, the one named last changes fastest.
Arguments:
- counts: int32 [32], P(('grp', 'sub')), may hold values from 1 to 3, as said below
- block_map: int32 [96], P(('grp', 'sub')), may hold values from 0 to 31
- perms: int32 [96, 256], P(('grp', 'sub')), may hold values from 0 to 255, each once within a row
- mass_ii: bfloat16 [96, 1024, 1024], P(('grp', 'sub')), may hold values from -0.005859375 to 0.005859375
- mass_ib: bfloat16 [96, 1024, 256], P(('grp', 'sub')), may hold values from -0.1875 to 0.1875
- mass_bb: bfloat16 [96, 256, 256], P(('grp', 'sub')), may hold values from -6 to 6
- constraint_modes: bfloat16 [96, 1024, 256], P(('grp', 'sub')), may hold values from -6 to 6
- fixed_modes: bfloat16 [96, 1024, 128], P(('grp', 'sub')), may hold values from -6 to 6
Outputs:
- blocks: float32 [32, 256, 256], P('grp', 'sub')
- coupling: float32 [96, 128, 256], P(('grp', 'sub'))
Inputs may be any that keep to these rules, and one draw needn't show every extreme that they name: `counts`: at least one device uses all 3 slots and one uses a single slot.
All inputs are finite; a program needn't handle non-finite values.
Results may differ from a plain program's by a relative error of at most 0.0021.
Values sent between devices are 32-bit elements; how exact they have to be, the bound alone decides.
No kernel may reach another device: no remote copies, remote signals or barrier semaphores. Data moves between devices by JAX's collectives and lax.ppermute only.
A program may use at most 128 MiB of HBM per device.

v0:
```python
import jax
import jax.numpy as jnp
from jax import lax
from jax.sharding import PartitionSpec as P

NBG = 16


def shifted(value, axis, by):
    peers = lax.axis_size(axis)
    return lax.ppermute(value, axis, [(i, (i + by) % peers) for i in range(peers)])


def contract(left, right):
    return lax.dot_general(
        left, right, (((0,), (0,)), ((), ())), preferred_element_type=jnp.float32
    )


def reduce_slot(mass_ii, mass_ib, mass_bb, constraint_modes, fixed_modes):
    product = jnp.dot(mass_ii, constraint_modes, preferred_element_type=jnp.float32).astype(
        jnp.bfloat16
    )
    cross = contract(constraint_modes, mass_ib)
    reduced = contract(constraint_modes, product) + cross + cross.T + mass_bb.astype(jnp.float32)
    coupled = contract(fixed_modes, product) + contract(fixed_modes, mass_ib)
    return (reduced, coupled)


def per_device(counts, block_map, perms, mass_ii, mass_ib, mass_bb, constraint_modes, fixed_modes):
    width = mass_bb.shape[1]
    modes = fixed_modes.shape[2]
    slot_total = mass_ii.shape[0]
    used_count = counts[0]
    sub_size = lax.axis_size("sub")

    def pick(array, slot_index):
        return lax.dynamic_index_in_dim(array, slot_index, 0, keepdims=False)

    start_parts = jnp.zeros((slot_total, width, width), jnp.float32)
    carry_state = (start_parts, jnp.zeros((slot_total, modes, width), jnp.float32))
    for slot_index in range(slot_total):
        one_parts, one_coupling = carry_state
        reduced, coupled = reduce_slot(
            pick(mass_ii, slot_index),
            pick(mass_ib, slot_index),
            pick(mass_bb, slot_index),
            pick(constraint_modes, slot_index),
            pick(fixed_modes, slot_index),
        )
        active = (slot_index < used_count).astype(jnp.float32)
        perm_row = pick(perms, slot_index)
        inverse = (
            jnp.zeros((width,), jnp.int32).at[perm_row].set(jnp.arange(width, dtype=jnp.int32))
        )
        placed = reduced[inverse][:, inverse] * active
        one_parts = lax.dynamic_update_index_in_dim(one_parts, placed, slot_index, 0)
        one_coupling = lax.dynamic_update_index_in_dim(
            one_coupling, coupled * active, slot_index, 0
        )
        carry_state = (one_parts, one_coupling)
    parts, coupling = carry_state
    slot_ids = jnp.arange(slot_total, dtype=jnp.int32)
    active_col = (slot_ids < used_count).astype(jnp.float32)
    targets = jnp.arange(2 * NBG, dtype=jnp.int32)
    one_hot = (block_map[:, None] == targets[None, :]).astype(jnp.float32) * active_col[:, None]
    spread_hot = jnp.broadcast_to(one_hot[:, None, :], (slot_total, sub_size, 2 * NBG))
    rows_in, hot_in = (
        lax.all_to_all(parts, "sub", split_axis=1, concat_axis=0, tiled=True),
        lax.all_to_all(spread_hot, "sub", split_axis=1, concat_axis=0, tiled=True),
    )
    hot_flat = hot_in[:, 0, :]
    owned = jnp.einsum("rc,rab->cab", hot_flat, rows_in, precision=lax.Precision.HIGHEST)
    home_rows = owned[:NBG]
    ahead_rows = owned[NBG:]
    blocks = home_rows + shifted(ahead_rows, "grp", 1)
    return (blocks, coupling)


def solution(mesh):
    placed = (
        P(("grp", "sub")),
        P(("grp", "sub")),
        P(("grp", "sub"), None),
        P(("grp", "sub"), None, None),
        P(("grp", "sub"), None, None),
        P(("grp", "sub"), None, None),
        P(("grp", "sub"), None, None),
        P(("grp", "sub"), None, None),
    )
    return jax.shard_map(
        per_device,
        mesh=mesh,
        in_specs=placed,
        out_specs=(P("grp", "sub", None), P(("grp", "sub"), None, None)),
        check_vma=False,
    )
```

profile of v0, /device:TPU:11, one launch (start us, length us, event | category | flops | bytes accessed | tf_op | source)
XLA Modules:
  0.0 96.7 jit_solution(16782596118019003462)
XLA Ops:
  1.4 0.7 fusion.83
  2.1 0.6 broadcast_in_dim.40
  2.8 6.6 %all-to-all-start = ((f32[3,16,32]{2,0,1:T(4,128)}), f32[3,16,32]{2,0,1:T(4,128)}, u32[]{:S(2)}, u32[]{:S(2)}) async-start(f32[3,16,32]{2,0,1:T(4,128)} %broadcast_in_dim.40), calls=%async_computation | async-start | bytes 65536 | tf_op jit(solution)/shard_map/all_to_all | solution.py:70
  9.3 2.2 %fusion.50 = f32[256,256]{1,0:T(8,128)} fusion(bf16[3,1024,256]{2,1,0:T(8,128)(2,1)} %param.12, bf16[3,1024,256]{2,1,0:T(8,128)(2,1)} %param.14), kind=kOutput, calls=%fused_computation.62 | convolution fusion | flops 134217728 | bytes 1310720 | tf_op jit(solution)/shard_map/dot_general | solution.py:15
  11.6 2.1 %fusion.38 = f32[256,256]{1,0:T(8,128)} fusion(bf16[3,1024,256]{2,1,0:T(8,128)(2,1)} %param.12, bf16[3,1024,256]{2,1,0:T(8,128)(2,1)S(1)} %copy-done), kind=kOutput, calls=%fused_computation.50 | convolution fusion | flops 134217728 | bytes 1310720 | tf_op jit(solution)/shard_map/dot_general | solution.py:15
  13.7 1.5 %fusion.44 = f32[256,256]{1,0:T(8,128)S(1)} fusion(bf16[3,1024,256]{2,1,0:T(8,128)(2,1)} %param.12, bf16[3,1024,256]{2,1,0:T(8,128)(2,1)S(1)} %copy-done), kind=kOutput, calls=%fused_computation.56 | convolution fusion | flops 134217728 | bytes 1310720 | tf_op jit(solution)/shard_map/dot_general | solution.py:15
  15.2 2.8 %fusion.9 = bf16[1024,256]{1,0:T(8,128)(2,1)S(1)} fusion(bf16[3,1024,1024]{2,1,0:T(8,128)(2,1)} %param.11, bf16[3,1024,256]{2,1,0:T(8,128)(2,1)S(1)} %copy-done), kind=kOutput, calls=%fused_computation.18 | convolution fusion | flops 537133056 | bytes 3145728 | tf_op jit(solution)/shard_map/dot_general | solution.py:21
  18.0 0.7 fusion.15
  18.7 0.7 fusion.12
  19.5 1.4 %scatter_custom_fusion = s32[256]{0:T(256)S(1)} fusion(s32[256]{0:T(256)S(1)} %bitcast.172, s32[256]{0:T(256)S(1)} %iota.22, s32[]{:T(128)} %constant.74.clone.1), kind=kCustom, calls=%fused_computation.115 | custom fusion | bytes 1028 | tf_op jit(solution)/shard_map/scatter | solution.py:54
  20.9 1.4 %scatter_custom_fusion.1 = s32[256]{0:T(256)S(1)} fusion(s32[256]{0:T(256)S(1)} %bitcast.171, s32[256]{0:T(256)S(1)} %iota.23, s32[]{:T(128)} %constant.74.clone.1), kind=kCustom, calls=%fused_computation.113 | custom fusion | bytes 1028 | tf_op jit(solution)/shard_map/scatter | solution.py:54
  22.3 1.4 %scatter_custom_fusion.2 = s32[256]{0:T(256)S(1)} fusion(s32[256]{0:T(256)S(1)} %bitcast.170, s32[256]{0:T(256)S(1)} %iota.24, s32[]{:T(128)} %constant.74.clone.1), kind=kCustom, calls=%fused_computation.111 | custom fusion | bytes 1028 | tf_op jit(solution)/shard_map/scatter | solution.py:54
  23.8 0.8 copy.53
  24.6 1.8 %copy.57 = f32[256,256]{0,1:T(8,128)} copy(f32[256,256]{1,0:T(8,128)} %fusion.38) | data formatting | bytes 524288 | tf_op jit(solution)/shard_map/dot_general | solution.py:15
  26.5 1.8 %copy.49 = f32[256,256]{0,1:T(8,128)} copy(f32[256,256]{1,0:T(8,128)} %fusion.50) | data formatting | bytes 524288 | tf_op jit(solution)/shard_map/dot_general | solution.py:15
  28.3 1.7 %fusion.90 = (bf16[1,256,256]{2,1,0:T(8,128)(2,1)}, bf16[1,256,256]{2,1,0:T(8,128)(2,1)}, bf16[1,256,256]{2,1,0:T(8,128)(2,1)S(1)}) fusion(bf16[3,256,256]{2,1,0:T(8,128)(2,1)} %param.13), kind=kLoop, calls=%fused_computation.117 | loop fusion | bytes 786432 | tf_op jit(solution)/shard_map/jit(dynamic_index_in_dim)/dynamic_slice | solution.py:38
  30.0 1.7 %copy.78 = bf16[1,256,256]{1,2,0:T(8,128)(2,1)} copy(bf16[1,256,256]{2,1,0:T(8,128)(2,1)} %get-tuple-element.8) | data formatting | bytes 262144
  31.7 1.7 %copy.77 = bf16[1,256,256]{1,2,0:T(8,128)(2,1)} copy(bf16[1,256,256]{2,1,0:T(8,128)(2,1)} %get-tuple-element.9) | data formatting | bytes 262144
  33.3 0.7 copy.76
  34.1 2.0 %fusion.26 = f32[256,256]{0,1:T(8,128)} fusion(f32[256,256]{0,1:T(8,128)} %copy.49, bf16[1024,256]{1,0:T(8,128)(2,1)S(1)} %fusion.9, bf16[3,1024,256]{2,1,0:T(8,128)(2,1)S(1)} %copy-done, f32[256,256]{1,0:T(8,128)S(1)} %copy-done.4, bf16[1,256,256]{1,2,0:T(8,128)(2,1)} %copy.76), kind=kOutput, calls=%fused_computation.32 | convolution fusion | flops 134479872 | bytes 1966080 | tf_op jit(solution)/shard_map/dot_general | solution.py:15
  36.1 1.1 %copy.51 = f32[256,256]{1,0:T(8,128)S(1)} copy(f32[256,256]{0,1:T(8,128)} %fusion.26) | data formatting | bytes 524288 | tf_op jit(solution)/shard_map/add | solution.py:25
  37.2 1.7 %gather_fusion = f32[256,256]{1,0:T(8,128)} fusion(f32[256,256]{1,0:T(8,128)S(1)} %copy.51, s32[1024]{0:T(1024)S(1)} %pad_clamp_fusion.2), kind=kCustom, calls=%fused_computation | custom fusion | bytes 525312 | tf_op jit(solution)/shard_map/gather | solution.py:56
  38.8 1.1 %copy.52 = f32[256,256]{0,1:T(8,128)S(1)} copy(f32[256,256]{1,0:T(8,128)} %gather_fusion) | data formatting | bytes 524288 | tf_op jit(solution)/shard_map/gather | solution.py:56
  40.0 1.7 %gather_fusion.1 = f32[256,256]{1,0:T(8,128)} fusion(f32[256,256]{0,1:T(8,128)S(1)} %copy.52, s32[1024]{0:T(1024)S(1)} %pad_clamp_fusion.2), kind=kCustom, calls=%fused_computation.1 | custom fusion | bytes 525312 | tf_op jit(solution)/shard_map/gather | solution.py:56
  41.6 2.1 %fusion.22 = f32[256,256]{0,1:T(8,128)} fusion(f32[256,256]{0,1:T(8,128)} %copy.57, bf16[1024,256]{1,0:T(8,128)(2,1)S(1)} %fusion.15, bf16[3,1024,256]{2,1,0:T(8,128)(2,1)S(1)} %copy-done, f32[256,256]{1,0:T(8,128)} %fusion.38, bf16[1,256,256]{1,2,0:T(8,128)(2,1)S(1)} %copy-done.8), kind=kOutput, calls=%fused_computation.28 | convolution fusion | flops 134479872 | bytes 1966080 | tf_op jit(solution)/shard_map/dot_general | solution.py:15
  43.7 1.1 %copy.59 = f32[256,256]{1,0:T(8,128)S(1)} copy(f32[256,256]{0,1:T(8,128)} %fusion.22) | data formatting | bytes 524288 | tf_op jit(solution)/shard_map/add | solution.py:25
  44.8 1.7 %gather_fusion.4 = f32[256,256]{1,0:T(8,128)} fusion(f32[256,256]{1,0:T(8,128)S(1)} %copy.59, s32[1024]{0:T(1024)S(1)} %pad_clamp_fusion), kind=kCustom, calls=%fused_computation.4 | custom fusion | bytes 525312 | tf_op jit(solution)/shard_map/gather | solution.py:56
  46.5 1.1 %copy.60 = f32[256,256]{0,1:T(8,128)S(1)} copy(f32[256,256]{1,0:T(8,128)} %gather_fusion.4) | data formatting | bytes 524288 | tf_op jit(solution)/shard_map/gather | solution.py:56
  47.6 1.7 %gather_fusion.5 = f32[256,256]{1,0:T(8,128)} fusion(f32[256,256]{0,1:T(8,128)S(1)} %copy.60, s32[1024]{0:T(1024)S(1)} %pad_clamp_fusion), kind=kCustom, calls=%fused_computation.5 | custom fusion | bytes 525312 | tf_op jit(solution)/shard_map/gather | solution.py:56
  49.2 1.4 %fusion.24 = f32[256,256]{0,1:T(8,128)S(1)} fusion(f32[256,256]{0,1:T(8,128)} %copy.53, bf16[1024,256]{1,0:T(8,128)(2,1)S(1)} %fusion.12, bf16[3,1024,256]{2,1,0:T(8,128)(2,1)S(1)} %copy-done, f32[256,256]{1,0:T(8,128)} %copy-done.3, bf16[1,256,256]{1,2,0:T(8,128)(2,1)S(1)} %copy-done.7), kind=kOutput, calls=%fused_computation.30 | convolution fusion | flops 134479872 | bytes 1966080 | tf_op jit(solution)/shard_map/dot_general | solution.py:15
  50.8 1.0 %gather_fusion.2 = f32[256,256]{1,0:T(8,128)S(1)} fusion(f32[256,256]{1,0:T(8,128)S(1)} %copy.55, s32[1024]{0:T(1024)S(1)} %pad_clamp_fusion.1), kind=kCustom, calls=%fused_computation.2 | custom fusion | bytes 525312 | tf_op jit(solution)/shard_map/gather | solution.py:56
  51.9 1.0 %gather_fusion.3 = f32[256,256]{1,0:T(8,128)S(1)} fusion(f32[256,256]{0,1:T(8,128)S(1)} %copy.56, s32[1024]{0:T(1024)S(1)} %pad_clamp_fusion.1), kind=kCustom, calls=%fused_computation.3 | custom fusion | bytes 525312 | tf_op jit(solution)/shard_map/gather | solution.py:56
  53.0 0.8 copy-done.2
  53.8 1.3 %copy.61 = f32[3,256,256]{2,0,1:T(4,128)} copy(f32[3,256,256]{1,2,0:T(8,128)S(1)} %bitcast_dynamic-update-slice_fusion) | data formatting | bytes 1572864 | tf_op jit(solution)/shard_map/jit(dynamic_update_index_in_dim)/dynamic_update_slice | solution.py:57
  55.1 6.0 %all-to-all-start.1 = ((f32[3,256,256]{2,0,1:T(4,128)}), f32[3,256,256]{2,0,1:T(4,128)S(1)}, u32[]{:S(2)}, u32[]{:S(2)}) async-start(f32[3,256,256]{2,0,1:T(4,128)} %copy.61), calls=%async_computation.1 | async-start | bytes 2097152 | tf_op jit(solution)/shard_map/all_to_all | solution.py:69
  61.2 1.4 %convolution_bitcast_fusion.5 = f32[128,256]{0,1:T(8,128)S(1)} fusion(bf16[1024,256]{1,0:T(8,128)(2,1)S(1)} %fusion.9, bf16[3,1024,128]{2,1,0:T(8,128)(2,1)} %param.15), kind=kOutput, calls=%fused_computation.46 | convolution fusion | flops 67108864 | bytes 917504 | tf_op jit(solution)/shard_map/dot_general | solution.py:15
  62.5 1.5 %fusion.34 = f32[1,128,256]{1,2,0:T(8,128)S(1)} fusion(f32[128,256]{0,1:T(8,128)S(1)} %convolution_bitcast_fusion.5, bf16[3,1024,256]{2,1,0:T(8,128)(2,1)} %param.12, bf16[3,1024,128]{2,1,0:T(8,128)(2,1)} %param.15, f32[]{:T(128)S(6)} %convert_element_type.48), kind=kOutput, calls=%fused_computation.45 | convolution fusion | flops 67174400 | bytes 1048580 | tf_op jit(solution)/shard_map/dot_general | solution.py:15
  64.0 0.3 convolution_bitcast_fusion.4
  64.4 1.4 %fusion.32 = f32[3,128,256]{1,2,0:T(8,128)S(1)} fusion(f32[3,128,256]{1,2,0:T(8,128)S(1)} %dynamic_update_slice.23, f32[128,256]{0,1:T(8,128)S(1)} %convolution_bitcast_fusion.4, bf16[3,1024,256]{2,1,0:T(8,128)(2,1)} %param.12, bf16[3,1024,128]{2,1,0:T(8,128)(2,1)S(1)} %copy-done.5, f32[]{:T(128)S(6)} %convert_element_type.52), kind=kOutput, calls=%fused_computation.41 | convolution fusion | flops 67174400 | bytes 1048580 | tf_op jit(solution)/shard_map/dot_general | solution.py:15
  65.8 0.8 squeeze.60
  66.6 19.5 %all-to-all-done.1 = f32[3,256,256]{2,0,1:T(4,128)S(1)} async-done(((f32[3,256,256]{2,0,1:T(4,128)}), f32[3,256,256]{2,0,1:T(4,128)S(1)}, u32[]{:S(2)}, u32[]{:S(2)}) %all-to-all-start.1) | async-done | bytes 786464 | tf_op jit(solution)/shard_map/all_to_all | solution.py:69
  86.3 1.0 %fusion.35 = f32[32,16,256]{2,0,1:T(8,128)S(1)} fusion(f32[48,16,256]{2,1,0:T(8,128)S(1)} %bitcast.169, f32[48,32]{1,0:T(8,128)S(1)} %squeeze.60), kind=kOutput, calls=%fused_computation.47 | convolution fusion | flops 75497472 | bytes 1316864 | tf_op jit(solution)/shard_map/rc,rab->cab/dot_general | solution.py:73
  87.4 0.3 collective-permute-start
  87.7 0.3 convolution_bitcast_fusion.3
  88.0 1.4 %fusion.29 = f32[3,128,256]{1,2,0:T(8,128)S(1)} fusion(f32[3,128,256]{1,2,0:T(8,128)S(1)} %fusion.32, f32[128,256]{0,1:T(8,128)S(1)} %convolution_bitcast_fusion.3, bf16[3,1024,256]{2,1,0:T(8,128)(2,1)} %param.12, bf16[3,1024,128]{2,1,0:T(8,128)(2,1)S(1)} %copy-done.6, f32[]{:T(128)S(6)} %convert_element_type.56), kind=kOutput, calls=%fused_computation.36 | convolution fusion | flops 67174400 | bytes 1048580 | tf_op jit(solution)/shard_map/dot_general | solution.py:15
  89.4 0.9 copy.70
  90.4 5.4 %collective-permute-done = f32[16,16,256]{2,0,1:T(8,128)S(1)} collective-permute-done((f32[16,16,256]{2,0,1:T(8,128)S(1)}, f32[16,16,256]{2,0,1:T(8,128)S(1)}, u32[]{:S(2)}, u32[]{:S(2)}) %collective-permute-start) | collective-permute-done | bytes 262176 | tf_op jit(solution)/shard_map/ppermute | solution.py:11
  95.8 0.9 copy.69
  (43 shorter events, 0.8 us)
Async XLA Ops:
  0.6 10.9 %copy-start = (bf16[3,1024,256]{2,1,0:T(8,128)(2,1)S(1)}, bf16[3,1024,256]{2,1,0:T(8,128)(2,1)}, u32[]{:S(2)}) copy-start(bf16[3,1024,256]{2,1,0:T(8,128)(2,1)} %param.14) | copy-start | bytes 4718596
  2.8 52.4 %all-to-all-start = ((f32[3,16,32]{2,0,1:T(4,128)}), f32[3,16,32]{2,0,1:T(4,128)}, u32[]{:S(2)}, u32[]{:S(2)}) async-start(f32[3,16,32]{2,0,1:T(4,128)} %broadcast_in_dim.40), calls=%async_computation | async-start | bytes 65536 | tf_op jit(solution)/shard_map/all_to_all | solution.py:70
  13.7 4.3 %copy-start.10 = (bf16[3,1024,1024]{2,1,0:T(8,128)(2,1)S(1)}, bf16[3,1024,1024]{2,1,0:T(8,128)(2,1)}, u32[]{:S(2)}) copy-start(bf16[3,1024,1024]{2,1,0:T(8,128)(2,1)} %param.11) | copy-start | bytes 18874372
  15.2 8.6 %copy-start.3 = (f32[256,256]{1,0:T(8,128)}, f32[256,256]{1,0:T(8,128)S(1)}, u32[]{:S(2)}) copy-start(f32[256,256]{1,0:T(8,128)S(1)} %fusion.44) | copy-start | bytes 786436
  18.7 0.7 copy-start.9
  24.6 9.4 %copy-start.4 = (f32[256,256]{1,0:T(8,128)S(1)}, f32[256,256]{1,0:T(8,128)}, u32[]{:S(2)}) copy-start(f32[256,256]{1,0:T(8,128)} %fusion.50) | copy-start | bytes 786436
  38.8 2.8 %copy-start.8 = (bf16[1,256,256]{1,2,0:T(8,128)(2,1)S(1)}, bf16[1,256,256]{1,2,0:T(8,128)(2,1)}, u32[]{:S(2)}) copy-start(bf16[1,256,256]{1,2,0:T(8,128)(2,1)} %copy.78) | copy-start | bytes 393220
  46.5 2.8 %copy-start.7 = (bf16[1,256,256]{1,2,0:T(8,128)(2,1)S(1)}, bf16[1,256,256]{1,2,0:T(8,128)(2,1)}, u32[]{:S(2)}) copy-start(bf16[1,256,256]{1,2,0:T(8,128)(2,1)} %copy.77) | copy-start | bytes 393220
  51.7 1.1 %copy-start.1 = (f32[256,256]{1,0:T(8,128)S(1)}, f32[256,256]{1,0:T(8,128)}, u32[]{:S(2)}) copy-start(f32[256,256]{1,0:T(8,128)} %gather_fusion.1) | copy-start | bytes 786436
  52.9 1.0 copy-start.2
  55.1 30.9 %all-to-all-start.1 = ((f32[3,256,256]{2,0,1:T(4,128)}), f32[3,256,256]{2,0,1:T(4,128)S(1)}, u32[]{:S(2)}, u32[]{:S(2)}) async-start(f32[3,256,256]{2,0,1:T(4,128)} %copy.61), calls=%async_computation.1 | async-start | bytes 2097152 | tf_op jit(solution)/shard_map/all_to_all | solution.py:69
  61.2 2.9 %copy-start.5 = (bf16[3,1024,128]{2,1,0:T(8,128)(2,1)S(1)}, bf16[3,1024,128]{2,1,0:T(8,128)(2,1)}, u32[]{:S(2)}) copy-start(bf16[3,1024,128]{2,1,0:T(8,128)(2,1)} %param.15) | copy-start | bytes 2359300
  86.2 1.5 %copy-start.6 = (bf16[3,1024,128]{2,1,0:T(8,128)(2,1)S(1)}, bf16[3,1024,128]{2,1,0:T(8,128)(2,1)}, u32[]{:S(2)}) copy-start(bf16[3,1024,128]{2,1,0:T(8,128)(2,1)} %param.15) | copy-start | bytes 2359300
  87.4 8.4 %collective-permute-start = (f32[16,16,256]{2,0,1:T(8,128)S(1)}, f32[16,16,256]{2,0,1:T(8,128)S(1)}, u32[]{:S(2)}, u32[]{:S(2)}) collective-permute-start(f32[16,16,256]{2,0,1:T(8,128)S(1)} %slice.39), channel_id=1, source_target_pairs={{0,16},{16,0},{1,17},{17,1},{2,18},{18,2},{3,19},{19,3},{4,20},{20... | collective-permute-start | bytes 786440 | tf_op jit(solution)/shard_map/ppermute | solution.py:11
where the time goes:
time: 97.5 us; the launch traced here: 96.7 us
  local copies, waits for them, and re-layouts  33.3 us (34%)
  waiting for transfers between devices  24.9 us (26%)
  matrix products  22.8 us (23%)
  starting transfers between devices  12.9 us (13%)
  between operations  1.81 us (2%)
    all_to_all x1, waiting for transfers between devices, per_device(): lax.all_to_all(parts, 'sub', split_axis=1, concat_axis=0, tiled=True)  19.5 us
    dot_general x12, matrix products, contract(): lax.dot_general(left, right, (((0,), (0,)), ((), ())), preferred_element_...  17.6 us
    gather x9, local copies, waits for them, and re-layouts, per_device(): placed = reduced[inverse][:, inverse] * active  11 us
    unnamed x27, local copies, waits for them, and re-layouts  6.7 us
    all_to_all x1, starting transfers between devices, per_device(): lax.all_to_all(spread_hot, 'sub', split_axis=1, concat_axis=0, tiled=True)  6.58 us
    all_to_all x1, starting transfers between devices, per_device(): lax.all_to_all(parts, 'sub', split_axis=1, concat_axis=0, tiled=True)  6.01 us
    ppermute x1, waiting for transfers between devices, shifted(): lax.ppermute(value, axis, [(i, (i + by) % peers) for i in range(peers)])  5.41 us
    dot_general x3, local copies, waits for them, and re-layouts, contract(): lax.dot_general(left, right, (((0,), (0,)), ((), ())), preferred_element_...  4.45 us
  transfers between devices with their start and end apart: 3, of which 2 were waited for; matrix products, arithmetic and copies ran while one was open for 54% of the time, Pallas kernels for 0%

commit v1 on v0

--- a/solution.py
+++ b/solution.py
@@ -67,7 +67,12 @@
     spread_hot = jnp.broadcast_to(one_hot[:, None, :], (slot_total, sub_size, 2 * NBG))
     rows_in, hot_in = (
         lax.all_to_all(parts, "sub", split_axis=1, concat_axis=0, tiled=True),
-        lax.all_to_all(spread_hot, "sub", split_axis=1, concat_axis=0, tiled=True),
+        jnp.concatenate(
+            lax.all_to_all(
+                jnp.stack(jnp.split(spread_hot, lax.axis_size("sub"), axis=1)), "sub", 0, 0
+            ),
+            axis=0,
+        ),
     )
     hot_flat = hot_in[:, 0, :]
     owned = jnp.einsum("rc,rab->cab", hot_flat, rows_in, precision=lax.Precision.HIGHEST)

time: 97.5 us -> 102 us (1.046)
  the two profiles are of different devices: /device:TPU:11 before, /device:TPU:0 now
where the time goes in v1:
time: 102 us; the launch traced here: 101 us
  local copies, waits for them, and re-layouts  32.6 us (32%)
  waiting for transfers between devices  27.3 us (27%)
  matrix products  23.9 us (23%)
  starting transfers between devices  15.7 us (15%)
  between operations  1.71 us (2%)
    dot_general x12, matrix products, contract(): lax.dot_general(left, right, (((0,), (0,)), ((), ())), preferred_element_...  18.7 us
    all_to_all x1, waiting for transfers between devices, per_device(): lax.all_to_all(parts, 'sub', split_axis=1, concat_axis=0, tiled=True)  18.7 us
    gather x9, local copies, waits for them, and re-layouts, per_device(): placed = reduced[inverse][:, inverse] * active  11 us
    all_to_all x1, starting transfers between devices, per_device(): lax.all_to_all(parts, 'sub', split_axis=1, concat_axis=0, tiled=True)  7.41 us
    all_to_all x1, starting transfers between devices, per_device(): lax.all_to_all(jnp.stack(jnp.split(spread_hot, lax.axis_size('sub'), axis...  6.79 us
    unnamed x27, local copies, waits for them, and re-layouts  6.7 us
    all_to_all x1, waiting for transfers between devices, per_device(): lax.all_to_all(jnp.stack(jnp.split(spread_hot, lax.axis_size('sub'), axis...  4.85 us
    dot_general x3, local copies, waits for them, and re-layouts, contract(): lax.dot_general(left, right, (((0,), (0,)), ((), ())), preferred_element_...  4.46 us
  transfers between devices with their start and end apart: 3, of which 3 were waited for; matrix products, arithmetic and copies ran while one was open for 8% of the time, Pallas kernels for 0%

profile of v1, /device:TPU:0, one launch (start us, length us, event | category | flops | bytes accessed | tf_op | source)
XLA Modules:
  0.0 101.5 jit_solution(6272469465471775551)
XLA Ops:
  0.6 2.4 %fusion.50 = f32[256,256]{1,0:T(8,128)} fusion(bf16[3,1024,256]{2,1,0:T(8,128)(2,1)} %param.12, bf16[3,1024,256]{2,1,0:T(8,128)(2,1)} %param.14), kind=kOutput, calls=%fused_computation.62 | convolution fusion | flops 134217728 | bytes 1310720 | tf_op jit(solution)/shard_map/dot_general | solution.py:15
  3.0 2.1 %fusion.38 = f32[256,256]{1,0:T(8,128)} fusion(bf16[3,1024,256]{2,1,0:T(8,128)(2,1)} %param.12, bf16[3,1024,256]{2,1,0:T(8,128)(2,1)S(1)} %copy-done), kind=kOutput, calls=%fused_computation.50 | convolution fusion | flops 134217728 | bytes 1310720 | tf_op jit(solution)/shard_map/dot_general | solution.py:15
  5.1 1.5 %fusion.44 = f32[256,256]{1,0:T(8,128)S(1)} fusion(bf16[3,1024,256]{2,1,0:T(8,128)(2,1)} %param.12, bf16[3,1024,256]{2,1,0:T(8,128)(2,1)S(1)} %copy-done), kind=kOutput, calls=%fused_computation.56 | convolution fusion | flops 134217728 | bytes 1310720 | tf_op jit(solution)/shard_map/dot_general | solution.py:15
  6.6 2.8 %fusion.9 = bf16[1024,256]{1,0:T(8,128)(2,1)S(1)} fusion(bf16[3,1024,1024]{2,1,0:T(8,128)(2,1)} %param.11, bf16[3,1024,256]{2,1,0:T(8,128)(2,1)S(1)} %copy-done), kind=kOutput, calls=%fused_computation.18 | convolution fusion | flops 537133056 | bytes 3145728 | tf_op jit(solution)/shard_map/dot_general | solution.py:21
  9.4 0.7 fusion.15
  10.1 0.7 fusion.12
  11.6 1.4 %scatter_custom_fusion = s32[256]{0:T(256)S(1)} fusion(s32[256]{0:T(256)S(1)} %bitcast.169, s32[256]{0:T(256)S(1)} %iota.22, s32[]{:T(128)} %constant.74.clone.1), kind=kCustom, calls=%fused_computation.114 | custom fusion | bytes 1028 | tf_op jit(solution)/shard_map/scatter | solution.py:54
  13.0 1.4 %scatter_custom_fusion.1 = s32[256]{0:T(256)S(1)} fusion(s32[256]{0:T(256)S(1)} %bitcast.168, s32[256]{0:T(256)S(1)} %iota.23, s32[]{:T(128)} %constant.74.clone.1), kind=kCustom, calls=%fused_computation.112 | custom fusion | bytes 1028 | tf_op jit(solution)/shard_map/scatter | solution.py:54
  14.4 1.4 %scatter_custom_fusion.2 = s32[256]{0:T(256)S(1)} fusion(s32[256]{0:T(256)S(1)} %bitcast.167, s32[256]{0:T(256)S(1)} %iota.24, s32[]{:T(128)} %constant.74.clone.1), kind=kCustom, calls=%fused_computation.110 | custom fusion | bytes 1028 | tf_op jit(solution)/shard_map/scatter | solution.py:54
  15.9 0.8 copy.53
  16.7 1.8 %copy.57 = f32[256,256]{0,1:T(8,128)} copy(f32[256,256]{1,0:T(8,128)} %fusion.38) | data formatting | bytes 524288 | tf_op jit(solution)/shard_map/dot_general | solution.py:15
  18.6 1.8 %copy.49 = f32[256,256]{0,1:T(8,128)} copy(f32[256,256]{1,0:T(8,128)} %fusion.50) | data formatting | bytes 524288 | tf_op jit(solution)/shard_map/dot_general | solution.py:15
  20.3 1.7 %fusion.89 = (bf16[1,256,256]{2,1,0:T(8,128)(2,1)}, bf16[1,256,256]{2,1,0:T(8,128)(2,1)}, bf16[1,256,256]{2,1,0:T(8,128)(2,1)S(1)}) fusion(bf16[3,256,256]{2,1,0:T(8,128)(2,1)} %param.13), kind=kLoop, calls=%fused_computation.116 | loop fusion | bytes 786432 | tf_op jit(solution)/shard_map/jit(dynamic_index_in_dim)/dynamic_slice | solution.py:38
  22.1 1.7 %copy.78 = bf16[1,256,256]{1,2,0:T(8,128)(2,1)} copy(bf16[1,256,256]{2,1,0:T(8,128)(2,1)} %get-tuple-element.8) | data formatting | bytes 262144
  23.7 1.7 %copy.77 = bf16[1,256,256]{1,2,0:T(8,128)(2,1)} copy(bf16[1,256,256]{2,1,0:T(8,128)(2,1)} %get-tuple-element.9) | data formatting | bytes 262144
  25.4 0.7 copy.76
  26.1 2.0 %fusion.26 = f32[256,256]{0,1:T(8,128)} fusion(f32[256,256]{0,1:T(8,128)} %copy.49, bf16[1024,256]{1,0:T(8,128)(2,1)S(1)} %fusion.9, bf16[3,1024,256]{2,1,0:T(8,128)(2,1)S(1)} %copy-done, f32[256,256]{1,0:T(8,128)S(1)} %copy-done.4, bf16[1,256,256]{1,2,0:T(8,128)(2,1)} %copy.76), kind=kOutput, calls=%fused_computation.32 | convolution fusion | flops 134479872 | bytes 1966080 | tf_op jit(solution)/shard_map/dot_general | solution.py:15
  28.2 1.1 %copy.51 = f32[256,256]{1,0:T(8,128)S(1)} copy(f32[256,256]{0,1:T(8,128)} %fusion.26) | data formatting | bytes 524288 | tf_op jit(solution)/shard_map/add | solution.py:25
  29.2 1.7 %gather_fusion = f32[256,256]{1,0:T(8,128)} fusion(f32[256,256]{1,0:T(8,128)S(1)} %copy.51, s32[1024]{0:T(1024)S(1)} %pad_clamp_fusion.2), kind=kCustom, calls=%fused_computation | custom fusion | bytes 525312 | tf_op jit(solution)/shard_map/gather | solution.py:56
  30.9 1.1 %copy.52 = f32[256,256]{0,1:T(8,128)S(1)} copy(f32[256,256]{1,0:T(8,128)} %gather_fusion) | data formatting | bytes 524288 | tf_op jit(solution)/shard_map/gather | solution.py:56
  32.0 1.7 %gather_fusion.1 = f32[256,256]{1,0:T(8,128)} fusion(f32[256,256]{0,1:T(8,128)S(1)} %copy.52, s32[1024]{0:T(1024)S(1)} %pad_clamp_fusion.2), kind=kCustom, calls=%fused_computation.1 | custom fusion | bytes 525312 | tf_op jit(solution)/shard_map/gather | solution.py:56
  33.7 2.1 %fusion.22 = f32[256,256]{0,1:T(8,128)} fusion(f32[256,256]{0,1:T(8,128)} %copy.57, bf16[1024,256]{1,0:T(8,128)(2,1)S(1)} %fusion.15, bf16[3,1024,256]{2,1,0:T(8,128)(2,1)S(1)} %copy-done, f32[256,256]{1,0:T(8,128)} %fusion.38, bf16[1,256,256]{1,2,0:T(8,128)(2,1)S(1)} %copy-done.7), kind=kOutput, calls=%fused_computation.28 | convolution fusion | flops 134479872 | bytes 1966080 | tf_op jit(solution)/shard_map/dot_general | solution.py:15
  35.8 1.1 %copy.59 = f32[256,256]{1,0:T(8,128)S(1)} copy(f32[256,256]{0,1:T(8,128)} %fusion.22) | data formatting | bytes 524288 | tf_op jit(solution)/shard_map/add | solution.py:25
  36.9 1.7 %gather_fusion.4 = f32[256,256]{1,0:T(8,128)} fusion(f32[256,256]{1,0:T(8,128)S(1)} %copy.59, s32[1024]{0:T(1024)S(1)} %pad_clamp_fusion), kind=kCustom, calls=%fused_computation.4 | custom fusion | bytes 525312 | tf_op jit(solution)/shard_map/gather | solution.py:56
  38.5 1.1 %copy.60 = f32[256,256]{0,1:T(8,128)S(1)} copy(f32[256,256]{1,0:T(8,128)} %gather_fusion.4) | data formatting | bytes 524288 | tf_op jit(solution)/shard_map/gather | solution.py:56
  39.6 1.7 %gather_fusion.5 = f32[256,256]{1,0:T(8,128)} fusion(f32[256,256]{0,1:T(8,128)S(1)} %copy.60, s32[1024]{0:T(1024)S(1)} %pad_clamp_fusion), kind=kCustom, calls=%fused_computation.5 | custom fusion | bytes 525312 | tf_op jit(solution)/shard_map/gather | solution.py:56
  41.3 1.4 %fusion.24 = f32[256,256]{0,1:T(8,128)S(1)} fusion(f32[256,256]{0,1:T(8,128)} %copy.53, bf16[1024,256]{1,0:T(8,128)(2,1)S(1)} %fusion.12, bf16[3,1024,256]{2,1,0:T(8,128)(2,1)S(1)} %copy-done, f32[256,256]{1,0:T(8,128)} %copy-done.3, bf16[1,256,256]{1,2,0:T(8,128)(2,1)S(1)} %copy-done.6), kind=kOutput, calls=%fused_computation.30 | convolution fusion | flops 134479872 | bytes 1966080 | tf_op jit(solution)/shard_map/dot_general | solution.py:15
  42.8 1.0 gather_fusion.2
  43.9 1.0 gather_fusion.3
  45.1 0.8 copy-done.2
  45.9 1.3 %copy.61 = f32[3,256,256]{2,0,1:T(4,128)} copy(f32[3,256,256]{1,2,0:T(8,128)S(1)} %bitcast_dynamic-update-slice_fusion) | data formatting | bytes 1572864 | tf_op jit(solution)/shard_map/jit(dynamic_update_index_in_dim)/dynamic_update_slice | solution.py:57
  47.2 7.4 %all-to-all-start.1 = ((f32[3,256,256]{2,0,1:T(4,128)}), f32[3,256,256]{2,0,1:T(4,128)S(1)}, u32[]{:S(2)}, u32[]{:S(2)}) async-start(f32[3,256,256]{2,0,1:T(4,128)} %copy.61), calls=%async_computation.1 | async-start | bytes 2097152 | tf_op jit(solution)/shard_map/all_to_all | solution.py:69
  54.6 1.3 %convolution_bitcast_fusion.5 = f32[128,256]{0,1:T(8,128)S(1)} fusion(bf16[1024,256]{1,0:T(8,128)(2,1)S(1)} %fusion.9, bf16[3,1024,128]{2,1,0:T(8,128)(2,1)} %param.15), kind=kOutput, calls=%fused_computation.46 | convolution fusion | flops 67108864 | bytes 917504 | tf_op jit(solution)/shard_map/dot_general | solution.py:15
  55.9 1.5 %fusion.34 = f32[1,128,256]{1,2,0:T(8,128)S(1)} fusion(f32[128,256]{0,1:T(8,128)S(1)} %convolution_bitcast_fusion.5, bf16[3,1024,256]{2,1,0:T(8,128)(2,1)} %param.12, bf16[3,1024,128]{2,1,0:T(8,128)(2,1)} %param.15, f32[]{:T(128)S(6)} %convert_element_type.48), kind=kOutput, calls=%fused_computation.45 | convolution fusion | flops 67174400 | bytes 1048580 | tf_op jit(solution)/shard_map/dot_general | solution.py:15
  57.5 1.3 %convolution_bitcast_fusion.4 = f32[128,256]{0,1:T(8,128)S(1)} fusion(bf16[1024,256]{1,0:T(8,128)(2,1)S(1)} %fusion.12, bf16[3,1024,128]{2,1,0:T(8,128)(2,1)} %param.15), kind=kOutput, calls=%fused_computation.42 | convolution fusion | flops 67108864 | bytes 917504 | tf_op jit(solution)/shard_map/dot_general | solution.py:15
  58.8 18.7 %all-to-all-done.1 = f32[3,256,256]{2,0,1:T(4,128)S(1)} async-done(((f32[3,256,256]{2,0,1:T(4,128)}), f32[3,256,256]{2,0,1:T(4,128)S(1)}, u32[]{:S(2)}, u32[]{:S(2)}) %all-to-all-start.1) | async-done | bytes 786464 | tf_op jit(solution)/shard_map/all_to_all | solution.py:69
  77.5 0.6 stack.2
  78.1 6.8 %all-to-all-start = ((f32[16,3,1,32]{3,2,1,0:T(1,128)}), f32[16,3,1,32]{3,2,1,0:T(1,128)S(1)}, u32[]{:S(2)}, u32[]{:S(2)}) async-start(f32[16,3,1,32]{3,2,1,0:T(1,128)} %stack.2), calls=%async_computation | async-start | bytes 49152 | tf_op jit(solution)/shard_map/all_to_all | solution.py:71
  84.9 1.5 %fusion.32 = f32[3,128,256]{1,2,0:T(8,128)S(1)} fusion(f32[3,128,256]{1,2,0:T(8,128)S(1)} %dynamic_update_slice.23, f32[128,256]{0,1:T(8,128)S(1)} %convolution_bitcast_fusion.4, bf16[3,1024,256]{2,1,0:T(8,128)(2,1)} %param.12, bf16[3,1024,128]{2,1,0:T(8,128)(2,1)} %param.15, f32[]{:T(128)S(6)} %convert_element_type.52), kind=kOutput, calls=%fused_computation.41 | convolution fusion | flops 67174400 | bytes 1048580 | tf_op jit(solution)/shard_map/dot_general | solution.py:15
  86.4 0.2 copy.62
  86.7 4.9 %all-to-all-done = f32[16,3,1,32]{3,2,1,0:T(1,128)S(1)} async-done(((f32[16,3,1,32]{3,2,1,0:T(1,128)}), f32[16,3,1,32]{3,2,1,0:T(1,128)S(1)}, u32[]{:S(2)}, u32[]{:S(2)}) %all-to-all-start) | async-done | bytes 6176 | tf_op jit(solution)/shard_map/all_to_all | solution.py:71
  91.5 1.0 %fusion.35 = f32[32,16,256]{2,0,1:T(8,128)S(1)} fusion(f32[48,32,1]{1,0,2:T(8,128)S(1)} %bitcast.166, f32[48,16,256]{2,1,0:T(8,128)S(1)} %bitcast.165), kind=kOutput, calls=%fused_computation.47 | convolution fusion | flops 75497472 | bytes 1316864 | tf_op jit(solution)/shard_map/rc,rab->cab/dot_general | solution.py:78
  92.6 1.5 %collective-permute-start = (f32[16,16,256]{2,0,1:T(8,128)S(1)}, f32[16,16,256]{2,0,1:T(8,128)S(1)}, u32[]{:S(2)}, u32[]{:S(2)}) collective-permute-start(f32[16,16,256]{2,0,1:T(8,128)S(1)} %slice.39), channel_id=1, source_target_pairs={{0,16},{16,0},{1,17},{17,1},{2,18},{18,2},{3,19},{19,3},{4,20},{20... | collective-permute-start | bytes 786440 | tf_op jit(solution)/shard_map/ppermute | solution.py:11
  94.1 0.3 convolution_bitcast_fusion.3
  94.5 1.4 %fusion.29 = f32[3,128,256]{1,2,0:T(8,128)S(1)} fusion(f32[3,128,256]{1,2,0:T(8,128)S(1)} %fusion.32, f32[128,256]{0,1:T(8,128)S(1)} %convolution_bitcast_fusion.3, bf16[3,1024,256]{2,1,0:T(8,128)(2,1)} %param.12, bf16[3,1024,128]{2,1,0:T(8,128)(2,1)S(1)} %copy-done.5, f32[]{:T(128)S(6)} %convert_element_type.56), kind=kOutput, calls=%fused_computation.36 | convolution fusion | flops 67174400 | bytes 1048580 | tf_op jit(solution)/shard_map/dot_general | solution.py:15
  95.9 0.9 copy.70
  96.8 3.8 %collective-permute-done = f32[16,16,256]{2,0,1:T(8,128)S(1)} collective-permute-done((f32[16,16,256]{2,0,1:T(8,128)S(1)}, f32[16,16,256]{2,0,1:T(8,128)S(1)}, u32[]{:S(2)}, u32[]{:S(2)}) %collective-permute-start) | collective-permute-done | bytes 262176 | tf_op jit(solution)/shard_map/ppermute | solution.py:11
  100.6 0.9 copy.69
  (42 shorter events, 0.7 us)
Async XLA Ops:
  0.6 2.4 %copy-start = (bf16[3,1024,256]{2,1,0:T(8,128)(2,1)S(1)}, bf16[3,1024,256]{2,1,0:T(8,128)(2,1)}, u32[]{:S(2)}) copy-start(bf16[3,1024,256]{2,1,0:T(8,128)(2,1)} %param.14) | copy-start | bytes 4718596
  5.1 4.3 %copy-start.10 = (bf16[3,1024,1024]{2,1,0:T(8,128)(2,1)S(1)}, bf16[3,1024,1024]{2,1,0:T(8,128)(2,1)}, u32[]{:S(2)}) copy-start(bf16[3,1024,1024]{2,1,0:T(8,128)(2,1)} %param.11) | copy-start | bytes 18874372
  6.6 9.3 %copy-start.3 = (f32[256,256]{1,0:T(8,128)}, f32[256,256]{1,0:T(8,128)S(1)}, u32[]{:S(2)}) copy-start(f32[256,256]{1,0:T(8,128)S(1)} %fusion.44) | copy-start | bytes 786436
  10.1 1.4 %copy-start.8 = (s32[3,256]{1,0:T(4,128)S(1)}, s32[3,256]{1,0:T(4,128)}, u32[]{:S(2)}) copy-start(s32[3,256]{1,0:T(4,128)} %param.10) | copy-start | bytes 9220
  16.7 9.4 %copy-start.4 = (f32[256,256]{1,0:T(8,128)S(1)}, f32[256,256]{1,0:T(8,128)}, u32[]{:S(2)}) copy-start(f32[256,256]{1,0:T(8,128)} %fusion.50) | copy-start | bytes 786436
  30.9 2.8 %copy-start.7 = (bf16[1,256,256]{1,2,0:T(8,128)(2,1)S(1)}, bf16[1,256,256]{1,2,0:T(8,128)(2,1)}, u32[]{:S(2)}) copy-start(bf16[1,256,256]{1,2,0:T(8,128)(2,1)} %copy.78) | copy-start | bytes 393220
  38.5 2.8 %copy-start.6 = (bf16[1,256,256]{1,2,0:T(8,128)(2,1)S(1)}, bf16[1,256,256]{1,2,0:T(8,128)(2,1)}, u32[]{:S(2)}) copy-start(bf16[1,256,256]{1,2,0:T(8,128)(2,1)} %copy.77) | copy-start | bytes 393220
  43.8 1.1 %copy-start.1 = (f32[256,256]{1,0:T(8,128)S(1)}, f32[256,256]{1,0:T(8,128)}, u32[]{:S(2)}) copy-start(f32[256,256]{1,0:T(8,128)} %gather_fusion.1) | copy-start | bytes 786436
  44.9 1.0 copy-start.2
  47.2 30.3 %all-to-all-start.1 = ((f32[3,256,256]{2,0,1:T(4,128)}), f32[3,256,256]{2,0,1:T(4,128)S(1)}, u32[]{:S(2)}, u32[]{:S(2)}) async-start(f32[3,256,256]{2,0,1:T(4,128)} %copy.61), calls=%async_computation.1 | async-start | bytes 2097152 | tf_op jit(solution)/shard_map/all_to_all | solution.py:69
  54.6 2.8 %copy-start.9 = (s32[3]{0:T(128)S(1)}, s32[3]{0:T(128)}, u32[]{:S(2)}) copy-start(s32[3]{0:T(128)} %param.9) | copy-start | bytes 40
  78.1 13.4 %all-to-all-start = ((f32[16,3,1,32]{3,2,1,0:T(1,128)}), f32[16,3,1,32]{3,2,1,0:T(1,128)S(1)}, u32[]{:S(2)}, u32[]{:S(2)}) async-start(f32[16,3,1,32]{3,2,1,0:T(1,128)} %stack.2), calls=%async_computation | async-start | bytes 49152 | tf_op jit(solution)/shard_map/all_to_all | solution.py:71
  86.6 7.5 %copy-start.5 = (bf16[3,1024,128]{2,1,0:T(8,128)(2,1)S(1)}, bf16[3,1024,128]{2,1,0:T(8,128)(2,1)}, u32[]{:S(2)}) copy-start(bf16[3,1024,128]{2,1,0:T(8,128)(2,1)} %param.15) | copy-start | bytes 2359300
  92.6 8.0 %collective-permute-start = (f32[16,16,256]{2,0,1:T(8,128)S(1)}, f32[16,16,256]{2,0,1:T(8,128)S(1)}, u32[]{:S(2)}, u32[]{:S(2)}) collective-permute-start(f32[16,16,256]{2,0,1:T(8,128)S(1)} %slice.39), channel_id=1, source_target_pairs={{0,16},{16,0},{1,17},{17,1},{2,18},{18,2},{3,19},{19,3},{4,20},{20... | collective-permute-start | bytes 786440 | tf_op jit(solution)/shard_map/ppermute | solution.py:11
